TPU v7x, 128 devices: a whole 4x4x4 slice. The times are simulated.
128 devices in a mesh: dp: 1, col: 2 (over core), row: 64 (over z, y, x).
Axes of the slice: x: 4, y: 4, z: 4, core: 2. Of those that a mesh axis runs over, the one named last changes fastest.
Arguments:
- images: bfloat16 [16, 512, 256, 256], P('dp', 'row', 'col')
- w_down1: bfloat16 [3, 3, 256, 512], replicated
- b_down1: float32 [512], replicated
- w_refine1: bfloat16 [3, 3, 512, 512], replicated
- b_refine1: float32 [512], replicated
- w_down2: bfloat16 [3, 3, 512, 1024], replicated
- b_down2: float32 [1024], replicated
- w_refine2: bfloat16 [3, 3, 1024, 1024], replicated
- b_refine2: float32 [1024], replicated
- w_down3: bfloat16 [3, 3, 1024, 2048], replicated
- b_down3: float32 [2048], replicated
- w_refine3: bfloat16 [3, 3, 2048, 2048], replicated
- b_refine3: float32 [2048], replicated
Outputs:
- output: bfloat16 [16, 64, 32, 2048], P('dp', 'row', 'col')
All inputs are finite; a program needn't handle non-finite values.
Results may differ from a plain program's by a relative error of at most 0.00847578.
Values are sent between devices in bfloat16 or wider.
A program may use at most 1 GiB of HBM per device.

v0:
```python
import jax
import jax.numpy as jnp
from jax import lax
from jax.experimental import pallas as pl
from jax.experimental.pallas import tpu as pltpu
from jax.sharding import PartitionSpec as P

MESH = pl.DeviceIdType.MESH
BF16 = jnp.bfloat16
F32 = jnp.float32
VM = pltpu.VMEM
SEM = pltpu.SemaphoreType.DMA
ANY_SPEC = pl.BlockSpec(memory_space=pl.ANY)
VM_SPEC = pl.BlockSpec(memory_space=VM)
PARAMS = pltpu.CompilerParams(has_side_effects=True, vmem_limit_bytes=63 * 2**20)


def loop(count, fn):
    def body(step, carry):
        fn(step)
        return carry

    lax.fori_loop(0, count, body, 0)


def down_one_kernel(row_size, img_hbm, w_ref, b_ref, out_hbm, inb, halo, colb, corn, frow, xbuf, ybuf, in_sem, halo_send, halo_recv, col_sem, corn_sem, y_send, y_recv, self_sem):
    col = lax.axis_index("col")
    row = lax.axis_index("row")
    x = lax.rem(row, 4)
    base_row = row - x

    def image_of(step, xpos):
        group = lax.rem(xpos + 6 - lax.rem(step, 4), 4)
        return 4 * group + 2 * (step // 4)

    def load(step):
        slot = lax.rem(step, 2)
        return pltpu.make_async_copy(img_hbm.at[pl.ds(image_of(step, x), 2)], inb.at[slot], in_sem.at[slot])

    def halo_copy(step):
        first = image_of(step, lax.rem(x + 1, 4))
        return pltpu.make_async_remote_copy(img_hbm.at[pl.ds(first, 2), 7], halo.at[step], halo_send.at[step], halo_recv.at[step], device_id={"row": row + 1}, device_id_type=MESH)

    def col_copy():
        return pltpu.make_async_remote_copy(img_hbm.at[:, :, pl.ds(112, 16)], colb, col_sem.at[0], col_sem.at[1], device_id={"col": 1}, device_id_type=MESH)

    def corn_copy():
        return pltpu.make_async_remote_copy(img_hbm.at[:, 7, pl.ds(112, 16)], corn, corn_sem.at[0], corn_sem.at[1], device_id={"col": 1, "row": row + 1}, device_id_type=MESH)

    load(0).start()

    @pl.when(col == 0)
    def _():
        col_copy().start()

    @pl.when(row < row_size - 1)
    def _():
        @pl.when(col == 0)
        def _():
            corn_copy().start()

        def body(step):
            halo_copy(step).start()

        loop(8, body)

    @pl.when(col == 0)
    def _():
        colb[...] = jnp.zeros_like(colb)

    @pl.when(jnp.logical_or(col == 0, row == 0))
    def _():
        corn[...] = jnp.zeros_like(corn)

    @pl.when(row == 0)
    def _():
        halo[...] = jnp.zeros_like(halo)

    @pl.when(col == 1)
    def _():
        col_copy().wait_recv()

        @pl.when(row > 0)
        def _():
            corn_copy().wait_recv()

    def taps(i, q, left, line):
        for h in range(2):
            lanes = slice(128 * h, 128 * h + 128)
            frow[h, 0:16] = left[:, lanes].astype(F32)
            frow[h, 16:144] = line[:, lanes].astype(F32)
        for t in range(3):
            for h in range(2):
                xbuf[i, q, :, 256 * t + 128 * h : 256 * t + 128 * h + 128] = frow[h, pl.ds(15 + t, 64, stride=2)].astype(BF16)

    def y_copy(step, i):
        half = step // 4
        group = lax.rem(x + 6 - lax.rem(step, 4), 4)
        dst = out_hbm.at[half, pl.ds(4 * x, 4), pl.ds(pl.multiple_of(64 * col, 64), 64)]
        return pltpu.make_async_remote_copy(ybuf.at[step, i], dst, y_send.at[step * 2 + i], y_recv.at[half * 8 + 2 * x + col], device_id={"col": i, "row": base_row + group}, device_id_type=MESH)

    def y_local(half):
        dst = out_hbm.at[half, pl.ds(4 * x, 4), pl.ds(pl.multiple_of(64 * col, 64), 64)]
        return pltpu.make_async_copy(ybuf.at[4 * half + 2, col], dst, self_sem.at[half])

    def main(step):
        slot = lax.rem(step, 2)
        first = image_of(step, x)

        @pl.when(step < 7)
        def _():
            load(step + 1).start()

        load(step).wait()

        @pl.when(row > 0)
        def _():
            halo_copy(step).wait_recv()

        for i in range(2):
            taps(i, 0, corn[first + i], halo[step, i])

            def line(q, i=i):
                taps(i, q + 1, colb[first + i, q], inb[slot, i, q])

            loop(8, line)
        acc = None
        for dy in range(3):
            lhs = jnp.concatenate([xbuf[i, 2 * o + dy] for i in range(2) for o in range(4)], axis=0)
            part = jnp.dot(lhs, w_ref[dy], preferred_element_type=F32)
            acc = part if acc is None else acc + part
        out = jnp.maximum(acc + b_ref[...], 0.0).astype(BF16)
        for i in range(2):
            for o in range(4):
                ybuf[step, i, o] = out[(4 * i + o) * 64 : (4 * i + o + 1) * 64]
        for i in range(2):
            here = jnp.logical_and(lax.rem(step, 4) == 2, col == i)

            @pl.when(here)
            def _():
                y_local(step // 4).start()

            @pl.when(jnp.logical_not(here))
            def _(i=i):
                y_copy(step, i).start()

    loop(8, main)

    def finish(step):
        for i in range(2):
            here = jnp.logical_and(lax.rem(step, 4) == 2, col == i)

            @pl.when(here)
            def _():
                y_local(step // 4).wait()

            @pl.when(jnp.logical_not(here))
            def _(i=i):
                y_copy(step, i).wait_send()

        half = step // 4
        src_x = lax.rem(step, 4)
        for i in range(2):
            @pl.when(jnp.logical_or(src_x != x, col != i))
            def _(i=i):
                dst = out_hbm.at[half, pl.ds(4 * src_x, 4), pl.ds(64 * i, 64)]
                pltpu.make_async_remote_copy(ybuf.at[0, 0], dst, y_send.at[0], y_recv.at[half * 8 + 2 * src_x + i], device_id={"col": i, "row": base_row + src_x}, device_id_type=MESH).wait_recv()

        @pl.when(row < row_size - 1)
        def _():
            halo_copy(step).wait_send()


    loop(8, finish)

    @pl.when(col == 0)
    def _():
        col_copy().wait_send()

        @pl.when(row < row_size - 1)
        def _():
            corn_copy().wait_send()


def down_one(row_size, images, w, b):
    def kernel(*refs):
        down_one_kernel(row_size, *refs)

    return pl.pallas_call(
        kernel,
        out_shape=jax.ShapeDtypeStruct((2, 16, 128, 512), BF16),
        in_specs=[ANY_SPEC, VM_SPEC, VM_SPEC],
        out_specs=ANY_SPEC,
        scratch_shapes=[
            VM((2, 2, 8, 128, 256), BF16),
            VM((8, 2, 128, 256), BF16),
            VM((16, 8, 16, 256), BF16),
            VM((16, 16, 256), BF16),
            VM((2, 144, 128), F32),
            VM((2, 9, 64, 768), BF16),
            VM((8, 2, 4, 64, 512), BF16),
            SEM((2,)),
            SEM((8,)),
            SEM((8,)),
            SEM((2,)),
            SEM((2,)),
            SEM((16,)),
            SEM((16,)),
            SEM((2,)),
        ],
        compiler_params=PARAMS,
        name="down_one",
    )(images, w.reshape(3, 768, 512), b.reshape(1, 512))


def shifted(value, by, width):
    size = value.shape[0]
    pos = lax.rem(lax.broadcasted_iota(jnp.int32, (size, 1), 0), width)
    edge = 0 if by == 1 else width - 1
    return jnp.where(pos == edge, 0.0, pltpu.roll(value, by % size, 0))


def split_columns(value, scratch, even_ref, odd_ref, index, lane, rows, width):
    half = width // 2
    for h in range(2):
        scratch[h] = value[:, 128 * h : 128 * h + 128]
        lanes = pl.ds(pl.multiple_of(lane + 128 * h, 128), 128)
        for ref, start in ((even_ref, 0), (odd_ref, 1)):
            part = scratch[h, pl.ds(start, rows * half, stride=2)].astype(BF16)
            ref[index[0], index[1], :, lanes] = part.reshape(rows, half, 128)


def middle_kernel(row_size, y1_hbm, w1_hbm, w2_hbm, w3_hbm, b1_ref, b2_ref, b3_ref, even2, odd2, y1v, w1, w2, w3, even1, odd1, y2v, scratch, w_sem, in_sem, ha_s, ha_r, hb_s, hb_r, hc_s, hc_r, hd_s, hd_r):
    row = lax.axis_index("row")
    has_up = row >= 4
    has_down = row < row_size - 4

    def remote(src, dst, send, recv, delta):
        return pltpu.make_async_remote_copy(src, dst, send, recv, device_id={"row": row + delta}, device_id_type=MESH)

    def halo1_down(i):
        return remote(y1_hbm.at[i, 15], y1v.at[i, 0], ha_s.at[i], ha_r.at[i], 4)

    def halo1_up(i):
        return remote(y1_hbm.at[i, 0], y1v.at[i, 17], ha_s.at[2 + i], ha_r.at[2 + i], -4)

    def halo2(i, which):
        ref = (even1, odd1)[which]
        return remote(ref.at[i, 16], ref.at[i, 0], hb_s.at[2 * i + which], hb_r.at[2 * i + which], 4)

    def halo3_down(i):
        return remote(y2v.at[i, 8], y2v.at[i, 0], hc_s.at[i], hc_r.at[i], 4)

    def halo3_up(i):
        return remote(y2v.at[i, 1], y2v.at[i, 9], hc_s.at[2 + i], hc_r.at[2 + i], -4)

    def halo4(i, which):
        ref = (even2, odd2)[which]
        return remote(ref.at[i, 8], ref.at[i, 0], hd_s.at[2 * i + which], hd_r.at[2 * i + which], 4)

    loads = [pltpu.make_async_copy(y1_hbm.at[i], y1v.at[i, pl.ds(1, 16)], in_sem.at[i]) for i in range(2)]
    weights = [pltpu.make_async_copy(src, dst, w_sem.at[n]) for n, (src, dst) in enumerate(((w1_hbm, w1), (w2_hbm, w2), (w3_hbm, w3)))]

    @pl.when(has_down)
    def _():
        for i in range(2):
            halo1_down(i).start()

    @pl.when(has_up)
    def _():
        for i in range(2):
            halo1_up(i).start()

    weights[0].start()
    for i in range(2):
        loads[i].start()

    @pl.when(jnp.logical_not(has_up))
    def _():
        for i in range(2):
            for ref in (y1v, even1, odd1, y2v, even2, odd2):
                ref[i, 0] = jnp.zeros(ref.shape[2:], BF16)

    @pl.when(jnp.logical_not(has_down))
    def _():
        for i in range(2):
            y1v[i, 17] = jnp.zeros(y1v.shape[2:], BF16)
            y2v[i, 9] = jnp.zeros(y2v.shape[2:], BF16)

    for i in range(2):
        loads[i].wait()
    weights[0].wait()

    def refine_block(src, i, first, rows, w, lanes):
        width = src.shape[2]
        m = rows * width
        lhs = jnp.concatenate([src[i, pl.ds(first + dy, rows)].reshape(m, -1) for dy in range(3)], axis=1)
        parts = []
        for dx in range(3):
            rhs = jnp.concatenate([w[dy, dx, :, lanes] for dy in range(3)], axis=0)
            parts.append(jnp.dot(lhs, rhs, preferred_element_type=F32))
        return parts[1] + shifted(parts[0], 1, width) + shifted(parts[2], -1, width)

    def stage_r1(step):
        i = lax.rem(step, 2)
        block = lax.rem(1 + step // 2, 4)
        for n in (1, 2):
            @pl.when(step == n)
            def _(n=n):
                weights[n].start()

        @pl.when(step == 4)
        def _():
            @pl.when(has_down)
            def _():
                for k in range(2):
                    halo1_up(k).wait_recv()

            @pl.when(has_up)
            def _():
                for k in range(2):
                    halo1_down(k).wait_recv()

        def chunk(n):
            lanes = pl.ds(pl.multiple_of(n * 256, 256), 256)
            out = refine_block(y1v, i, 4 * block, 4, w1, lanes)
            out = jnp.maximum(out + b1_ref[:, lanes], 0.0)
            split_columns(out, scratch, even1, odd1, (i, pl.ds(1 + 4 * block, 4)), n * 256, 4, 128)

        loop(2, chunk)

        @pl.when(jnp.logical_and(has_down, block == 3))
        def _():
            for which in range(2):
                halo2(i, which).start()


    loop(8, stage_r1)
    weights[1].wait()

    def stage_d2(i):
        @pl.when(has_up)
        def _():
            for which in range(2):
                halo2(i, which).wait_recv()

        def chunk(n):
            lanes = pl.ds(pl.multiple_of(n * 256, 256), 256)

            def gather(ref):
                return [jnp.concatenate([ref[i, 2 * o + dy] for o in range(8)], axis=0) for dy in range(3)]

            odd = gather(odd1)
            both = jnp.concatenate(gather(even1) + odd, axis=1)
            rhs = jnp.concatenate([w2[dy, dx, :, lanes] for dx in (1, 2) for dy in range(3)], axis=0)
            left = jnp.concatenate([w2[dy, 0, :, lanes] for dy in range(3)], axis=0)
            out = jnp.dot(both, rhs, preferred_element_type=F32)
            out = out + shifted(jnp.dot(jnp.concatenate(odd, axis=1), left, preferred_element_type=F32), 1, 64)
            out = jnp.maximum(out + b2_ref[:, lanes], 0.0).astype(BF16)
            y2v[i, 1:9, :, lanes] = out.reshape(8, 64, 256)

        loop(4, chunk)

        @pl.when(has_down)
        def _():
            halo3_down(i).start()

        @pl.when(has_up)
        def _():
            halo3_up(i).start()


    loop(2, stage_d2)
    weights[2].wait()

    def stage_r2(i):
        @pl.when(has_up)
        def _():
            halo3_down(i).wait_recv()

        @pl.when(has_down)
        def _():
            halo3_up(i).wait_recv()

        def chunk(n):
            lanes = pl.ds(pl.multiple_of(n * 256, 256), 256)
            out = refine_block(y2v, i, 0, 8, w3, lanes)
            out = jnp.maximum(out + b3_ref[:, lanes], 0.0)
            split_columns(out, scratch, even2, odd2, (i, pl.ds(1, 8)), n * 256, 8, 64)

        loop(4, chunk)

        @pl.when(has_down)
        def _():
            for which in range(2):
                halo4(i, which).start()


    loop(2, stage_r2)

    @pl.when(has_down)
    def _():
        for i in range(2):
            halo1_down(i).wait_send()
            halo3_down(i).wait_send()
            for which in range(2):
                halo2(i, which).wait_send()
                halo4(i, which).wait_send()

    @pl.when(has_up)
    def _():
        for i in range(2):
            halo1_up(i).wait_send()
            halo3_up(i).wait_send()
            for which in range(2):
                halo4(i, which).wait_recv()


def middle(row_size, y1, w1, w2, w3, b1, b2, b3):
    def kernel(*refs):
        middle_kernel(row_size, *refs)

    return pl.pallas_call(
        kernel,
        out_shape=[jax.ShapeDtypeStruct((2, 9, 32, 1024), BF16)] * 2,
        in_specs=[ANY_SPEC] * 4 + [VM_SPEC] * 3,
        out_specs=[VM_SPEC] * 2,
        scratch_shapes=[
            VM((2, 18, 128, 512), BF16),
            VM((3, 3, 512, 512), BF16),
            VM((3, 3, 512, 1024), BF16),
            VM((3, 3, 1024, 1024), BF16),
            VM((2, 17, 64, 512), BF16),
            VM((2, 17, 64, 512), BF16),
            VM((2, 10, 64, 1024), BF16),
            VM((2, 512, 128), F32),
            SEM((3,)),
            SEM((2,)),
        ]
        + [SEM((4,))] * 8,
        compiler_params=PARAMS,
        name="middle",
    )(y1, w1, w2, w3, b1.reshape(1, -1), b2.reshape(1, -1), b3.reshape(1, -1))


RING = 4
WIDE = 512


def last_kernel(row_size, even2, odd2, w1_hbm, w2_hbm, b1_ref, b2_ref, out_hbm, w1, w2, y3v, obuf, lhs1, acc, w1_sem, w2_sem, up_s, up_r, down_s, down_r, o_s, o_r, self_sem):
    col = lax.axis_index("col")
    row = lax.axis_index("row")
    x = lax.rem(row, 4)
    base_row = row - x
    has_up = row >= 4
    has_down = row < row_size - 4
    total = 3 * (2048 // WIDE)

    def lanes_of(n):
        return pl.ds(pl.multiple_of(n * WIDE, WIDE), WIDE)

    def load(t, src, dst, sems):
        slot = lax.rem(t, RING)
        return pltpu.make_async_copy(src.at[:, lax.rem(t + 1, 3), :, lanes_of(t // 3)], dst.at[slot], sems.at[slot])

    def load1(t):
        return load(t, w1_hbm, w1, w1_sem)

    def load2(t):
        return load(t, w2_hbm, w2, w2_sem)

    def halo_up(n):
        return pltpu.make_async_remote_copy(y3v.at[:, 1, :, lanes_of(n)], y3v.at[:, 5, :, lanes_of(n)], up_s.at[n], up_r.at[n], device_id={"row": row - 4}, device_id_type=MESH)

    def halo_down(n):
        return pltpu.make_async_remote_copy(y3v.at[:, 4, :, lanes_of(n)], y3v.at[:, 0, :, lanes_of(n)], down_s.at[n], down_r.at[n], device_id={"row": row + 4}, device_id_type=MESH)

    def out_copy(n, xd, cd):
        dst = out_hbm.at[x, :, col, :, lanes_of(n)]
        return pltpu.make_async_remote_copy(obuf.at[n, :, xd, pl.ds(16 * cd, 16)], dst, o_s.at[n, 2 * xd + cd], o_r.at[n, 2 * x + col], device_id={"col": cd, "row": base_row + xd}, device_id_type=MESH)

    def out_recv(n, xs, cs):
        dst = out_hbm.at[xs, :, cs, :, lanes_of(n)]
        return pltpu.make_async_remote_copy(obuf.at[n, :, xs, pl.ds(16 * cs, 16)], dst, o_s.at[n, 2 * xs + cs], o_r.at[n, 2 * xs + cs], device_id={"col": cs, "row": base_row + xs}, device_id_type=MESH)

    def out_self(n):
        dst = out_hbm.at[x, :, col, :, lanes_of(n)]
        return pltpu.make_async_copy(obuf.at[n, :, x, pl.ds(pl.multiple_of(16 * col, 16), 16)], dst, self_sem.at[n])

    for t in range(RING - 1):
        load1(t).start()

    @pl.when(jnp.logical_not(has_up))
    def _():
        y3v[:, 0] = jnp.zeros((2, 32, 2048), BF16)

    @pl.when(jnp.logical_not(has_down))
    def _():
        y3v[:, 5] = jnp.zeros((2, 32, 2048), BF16)

    for k, ref in enumerate((even2, odd2)):
        for dy in range(3):
            for i in range(2):
                for o in range(4):
                    first = 32 * (4 * i + o)
                    lhs1[k, first : first + 32, 1024 * dy : 1024 * dy + 1024] = ref[i, 2 * o + dy]

    def stage_d3(t):
        load1(t).wait()
        ahead = t + RING - 1

        @pl.when(ahead < total)
        def _():
            load1(ahead).start()

        @pl.when(ahead >= total)
        def _():
            load2(ahead - total).start()

        j = lax.rem(t, 3)
        n = t // 3
        acc[j] = jnp.dot(lhs1[(j + 1) // 2], w1[lax.rem(t, RING)].reshape(3072, WIDE), preferred_element_type=F32)

        @pl.when(j == 2)
        def _():
            out = acc[0] + acc[1] + shifted(acc[2], 1, 32)
            out = jnp.maximum(out + b1_ref[:, lanes_of(n)], 0.0).astype(BF16)
            y3v[:, 1:5, :, lanes_of(n)] = out.reshape(2, 4, 32, WIDE)

            @pl.when(has_up)
            def _():
                halo_up(n).start()

            @pl.when(has_down)
            def _():
                halo_down(n).start()

    loop(total, stage_d3)

    def halo_wait(n):
        @pl.when(has_down)
        def _():
            halo_up(n).wait_recv()

        @pl.when(has_up)
        def _():
            halo_down(n).wait_recv()

    loop(total // 3, halo_wait)

    def stage_r3(t):
        load2(t).wait()
        ahead = t + RING - 1

        @pl.when(ahead < total)
        def _():
            load2(ahead).start()

        j = lax.rem(t, 3)
        n = t // 3
        lhs = jnp.concatenate([y3v[:, dy : dy + 4].reshape(256, 2048) for dy in range(3)], axis=1)
        acc[j] = jnp.dot(lhs, w2[lax.rem(t, RING)].reshape(6144, WIDE), preferred_element_type=F32)

        @pl.when(j == 2)
        def _():
            out = acc[0] + shifted(acc[1], -1, 32) + shifted(acc[2], 1, 32)
            out = jnp.maximum(out + b2_ref[:, lanes_of(n)], 0.0).astype(BF16)
            obuf[n] = out.reshape(2, 4, 32, WIDE)
            for xd in range(4):
                for cd in range(2):
                    here = jnp.logical_and(x == xd, col == cd)

                    @pl.when(here)
                    def _():
                        out_self(n).start()

                    @pl.when(jnp.logical_not(here))
                    def _(xd=xd, cd=cd):
                        out_copy(n, xd, cd).start()

    loop(total, stage_r3)

    def finish(n):
        out_self(n).wait()
        for xd in range(4):
            for cd in range(2):
                @pl.when(jnp.logical_or(x != xd, col != cd))
                def _(xd=xd, cd=cd):
                    out_copy(n, xd, cd).wait_send()
                    out_recv(n, xd, cd).wait_recv()

        @pl.when(has_up)
        def _():
            halo_up(n).wait_send()

        @pl.when(has_down)
        def _():
            halo_down(n).wait_send()

    loop(total // 3, finish)


def last(row_size, even2, odd2, w1, w2, b1, b2):
    def kernel(*refs):
        last_kernel(row_size, *refs)

    return pl.pallas_call(
        kernel,
        out_shape=jax.ShapeDtypeStruct((4, 2, 2, 16, 2048), BF16),
        in_specs=[VM_SPEC, VM_SPEC, ANY_SPEC, ANY_SPEC, VM_SPEC, VM_SPEC],
        out_specs=ANY_SPEC,
        scratch_shapes=[
            VM((RING, 3, 1024, WIDE), BF16),
            VM((RING, 3, 2048, WIDE), BF16),
            VM((2, 6, 32, 2048), BF16),
            VM((4, 2, 4, 32, WIDE), BF16),
            VM((2, 256, 3072), BF16),
            VM((3, 256, WIDE), F32),
        ]
        + [SEM((RING,))] * 6
        + [SEM((RING, 8))] * 2
        + [SEM((RING,))],
        compiler_params=PARAMS,
        name="last",
    )(even2, odd2, w1, w2, b1.reshape(1, -1), b2.reshape(1, -1))


def solution(mesh):
    row_size = mesh.shape["row"]

    def local_encoder(images, w_down1, b_down1, w_refine1, b_refine1, w_down2, b_down2, w_refine2, b_refine2, w_down3, b_down3, w_refine3, b_refine3):
        y = down_one(row_size, images, w_down1, b_down1)
        even, odd = middle(row_size, y, w_refine1, w_down2, w_refine2, b_refine1, b_down2, b_refine2)
        out = last(row_size, even, odd, w_down3, w_refine3, b_down3, b_refine3)
        return out.reshape(16, 1, 16, 2048)

    tile_spec = P("dp", "row", "col")
    return jax.shard_map(local_encoder, mesh=mesh, in_specs=(tile_spec,) + (P(),) * 12, out_specs=tile_spec, check_vma=False)
```

profile of v0, /device:TPU:1, one launch (start us, length us, event | category | flops | bytes accessed | tf_op | source)
XLA Modules:
  0.0 220.1 jit_solution(8739048467445422077)
XLA Ops:
  0.0 85.1 %down_one.1.refs_0_ = bf16[2,16,128,512]{3,2,1,0:T(8,128)(2,1)} custom-call(bf16[16,8,128,256]{3,2,1,0:T(8,128)(2,1)} %refs_0_.1, bf16[3,768,512]{2,1,0:T(8,128)(2,1)} %bitcast.11, f32[1,512]{1,0:T(1,128)} %bitcast.16), custom_call_target="tpu_custom_call" | custom-call | tf_op jit(solution)/shard_map/down_one/pallas_call | solution.py:189
  85.1 71.8 %middle.1 = (bf16[2,9,32,1024]{3,2,1,0:T(8,128)(2,1)}, bf16[2,9,32,1024]{3,2,1,0:T(8,128)(2,1)}) custom-call(bf16[2,16,128,512]{3,2,1,0:T(8,128)(2,1)} %down_one.1.refs_0_, bf16[3,3,512,512]{3,2,1,0:T(8,128)(2,1)} %refs_1_.1, bf16[3,3,512,1024]{3,2,1,0:T(8,128)(2,1)} %refs_2_.2, bf16[3,3,1024,1024]{3,2,1,0:T(8,128)(2,1)} %refs_3_.2, f32[1,512]{1,0:T(1,128)} %bitcast.17, ...), custom_call_target="tpu_custom_call" | custom-call | tf_op jit(solution)/shard_map/middle/pallas_call | solution.py:423
  156.9 60.8 %last.1 = bf16[4,2,2,16,2048]{4,3,2,1,0:T(8,128)(2,1)} custom-call(bf16[2,9,32,1024]{3,2,1,0:T(8,128)(2,1)} %get-tuple-element.7.refs_0_, bf16[2,9,32,1024]{3,2,1,0:T(8,128)(2,1)} %get-tuple-element.8.refs_1_, bf16[3,3,1024,2048]{3,2,1,0:T(8,128)(2,1)} %refs_2_.3, bf16[3,3,2048,2048]{3,2,1,0:T(8,128)(2,1)} %refs_3_.3, f32[1,2048]{1,0:T(1,128)} %bitcast.12, ...), custom_call_target="tpu_custom_call" | custom-call | tf_op jit(solution)/shard_map/last/pallas_call | solution.py:607
  217.8 2.3 %copy.16 = bf16[16,1,16,2048]{3,2,1,0:T(8,128)(2,1)} copy(bf16[16,1,16,2048]{3,2,1,0:T(8,128)(2,1)} %bitcast.10) | data formatting | bytes 2097152
where the time goes:
time: 220 us
  Pallas kernels  218 us (99%)
  local copies, waits for them, and re-layouts  2.3 us (1%)
    pallas_call x1, Pallas kernels, down_one(): pl.pallas_call(kernel, out_shape=jax.ShapeDtypeStruct((2, 16, 128, 512),...  85.1 us
    pallas_call x1, Pallas kernels, middle(): pl.pallas_call(kernel, out_shape=[jax.ShapeDtypeStruct((2, 9, 32, 1024),...  71.8 us
    pallas_call x1, Pallas kernels, last(): pl.pallas_call(kernel, out_shape=jax.ShapeDtypeStruct((4, 2, 2, 16, 2048)...  60.8 us

commit v1 on v0

--- a/solution.py
+++ b/solution.py
@@ -23,15 +23,38 @@
     lax.fori_loop(0, count, body, 0)
 
 
-def down_one_kernel(row_size, img_hbm, w_ref, b_ref, out_hbm, inb, halo, colb, corn, frow, xbuf, ybuf, in_sem, halo_send, halo_recv, col_sem, corn_sem, y_send, y_recv, self_sem):
+def shifted(value, by, width):
+    size = value.shape[0]
+    pos = lax.rem(lax.broadcasted_iota(jnp.int32, (size, 1), 0), width)
+    edge = 0 if by == 1 else width - 1
+    return jnp.where(pos == edge, 0.0, pltpu.roll(value, by % size, 0))
+
+
+def split_columns(value, scratch, even_ref, odd_ref, index, lane, rows, width):
+    half = width // 2
+    for h in range(2):
+        scratch[h] = value[:, 128 * h : 128 * h + 128]
+        lanes = pl.ds(pl.multiple_of(lane + 128 * h, 128), 128)
+        for ref, start in ((even_ref, 0), (odd_ref, 1)):
+            part = scratch[h, pl.ds(start, rows * half, stride=2)].astype(BF16)
+            ref[index[0], index[1], :, lanes] = part.reshape(rows, half, 128)
+
+
+def front_kernel(row_size, img_hbm, w0_ref, b0_ref, w1_hbm, w2_hbm, w3_hbm, b1_ref, b2_ref, b3_ref, even2, odd2, inb, halo, colb, corn, frow, xbuf, ybuf, y1v, w1, w2, w3, even1, odd1, y2v, scratch, in_sem, halo_send, halo_recv, col_sem, corn_sem, y_send, y_recv, self_sem, w_sem, ha_s, ha_r, hb_s, hb_r, hc_s, hc_r, hd_s, hd_r):
     col = lax.axis_index("col")
     row = lax.axis_index("row")
     x = lax.rem(row, 4)
     base_row = row - x
+    has_up = row >= 4
+    has_down = row < row_size - 4
+    sends_row = row < row_size - 1
+    weights = [pltpu.make_async_copy(src, dst, w_sem.at[n]) for n, (src, dst) in enumerate(((w1_hbm, w1), (w2_hbm, w2), (w3_hbm, w3)))]
+
+    def group_of(step, xpos):
+        return lax.rem(xpos + 6 - lax.rem(step, 4), 4)
 
     def image_of(step, xpos):
-        group = lax.rem(xpos + 6 - lax.rem(step, 4), 4)
-        return 4 * group + 2 * (step // 4)
+        return 4 * group_of(step, xpos) + 2 * (step // 4)
 
     def load(step):
         slot = lax.rem(step, 2)
@@ -47,13 +70,46 @@
     def corn_copy():
         return pltpu.make_async_remote_copy(img_hbm.at[:, 7, pl.ds(112, 16)], corn, corn_sem.at[0], corn_sem.at[1], device_id={"col": 1, "row": row + 1}, device_id_type=MESH)
 
+    def y_place(half, xs, cs):
+        return y1v.at[half, pl.ds(1 + 4 * xs, 4), pl.ds(pl.multiple_of(64 * cs, 64), 64)]
+
+    def y_copy(step, i):
+        half = step // 4
+        return pltpu.make_async_remote_copy(ybuf.at[step, i], y_place(half, x, col), y_send.at[step * 2 + i], y_recv.at[half * 8 + 2 * x + col], device_id={"col": i, "row": base_row + group_of(step, x)}, device_id_type=MESH)
+
+    def y_local(half):
+        return pltpu.make_async_copy(ybuf.at[4 * half + 2, col], y_place(half, x, col), self_sem.at[half])
+
+    def ring(src, dst, send, recv, delta):
+        return pltpu.make_async_remote_copy(src, dst, send, recv, device_id={"row": row + delta}, device_id_type=MESH)
+
+    def halo1_down(i):
+        return ring(y1v.at[i, 16], y1v.at[i, 0], ha_s.at[i], ha_r.at[i], 4)
+
+    def halo1_up(i):
+        return ring(y1v.at[i, 1], y1v.at[i, 17], ha_s.at[2 + i], ha_r.at[2 + i], -4)
+
+    def halo2(i, which):
+        ref = (even1, odd1)[which]
+        return ring(ref.at[i, 16], ref.at[i, 0], hb_s.at[2 * i + which], hb_r.at[2 * i + which], 4)
+
+    def halo3_down(i):
+        return ring(y2v.at[i, 8], y2v.at[i, 0], hc_s.at[i], hc_r.at[i], 4)
+
+    def halo3_up(i):
+        return ring(y2v.at[i, 1], y2v.at[i, 9], hc_s.at[2 + i], hc_r.at[2 + i], -4)
+
+    def halo4(i, which):
+        ref = (even2, odd2)[which]
+        return ring(ref.at[i, 8], ref.at[i, 0], hd_s.at[2 * i + which], hd_r.at[2 * i + which], 4)
+
     load(0).start()
 
     @pl.when(col == 0)
     def _():
         col_copy().start()
 
-    @pl.when(row < row_size - 1)
+    @pl.when(sends_row)
     def _():
         @pl.when(col == 0)
         def _():
@@ -75,6 +131,18 @@
     @pl.when(row == 0)
     def _():
         halo[...] = jnp.zeros_like(halo)
+
+    @pl.when(jnp.logical_not(has_up))
+    def _():
+        for i in range(2):
+            for ref in (y1v, even1, odd1, y2v, even2, odd2):
+                ref[i, 0] = jnp.zeros(ref.shape[2:], BF16)
+
+    @pl.when(jnp.logical_not(has_down))
+    def _():
+        for i in range(2):
+            y1v[i, 17] = jnp.zeros(y1v.shape[2:], BF16)
+            y2v[i, 9] = jnp.zeros(y2v.shape[2:], BF16)
 
     @pl.when(col == 1)
     def _():
@@ -93,23 +161,21 @@
             for h in range(2):
                 xbuf[i, q, :, 256 * t + 128 * h : 256 * t + 128 * h + 128] = frow[h, pl.ds(15 + t, 64, stride=2)].astype(BF16)
 
-    def y_copy(step, i):
-        half = step // 4
-        group = lax.rem(x + 6 - lax.rem(step, 4), 4)
-        dst = out_hbm.at[half, pl.ds(4 * x, 4), pl.ds(pl.multiple_of(64 * col, 64), 64)]
-        return pltpu.make_async_remote_copy(ybuf.at[step, i], dst, y_send.at[step * 2 + i], y_recv.at[half * 8 + 2 * x + col], device_id={"col": i, "row": base_row + group}, device_id_type=MESH)
-
-    def y_local(half):
-        dst = out_hbm.at[half, pl.ds(4 * x, 4), pl.ds(pl.multiple_of(64 * col, 64), 64)]
-        return pltpu.make_async_copy(ybuf.at[4 * half + 2, col], dst, self_sem.at[half])
-
-    def main(step):
+    def is_local(step, i):
+        return jnp.logical_and(lax.rem(step, 4) == 2, col == i)
+
+    def stage_d1(step):
         slot = lax.rem(step, 2)
         first = image_of(step, x)
 
         @pl.when(step < 7)
         def _():
             load(step + 1).start()
+
+        for n in range(3):
+            @pl.when(step == n + 1)
+            def _(n=n):
+                weights[n].start()
 
         load(step).wait()
 
@@ -127,14 +193,12 @@
         acc = None
         for dy in range(3):
             lhs = jnp.concatenate([xbuf[i, 2 * o + dy] for i in range(2) for o in range(4)], axis=0)
-            part = jnp.dot(lhs, w_ref[dy], preferred_element_type=F32)
+            part = jnp.dot(lhs, w0_ref[dy], preferred_element_type=F32)
             acc = part if acc is None else acc + part
-        out = jnp.maximum(acc + b_ref[...], 0.0).astype(BF16)
+        out = jnp.maximum(acc + b0_ref[...], 0.0).astype(BF16)
+        ybuf[step] = out.reshape(2, 4, 64, 512)
         for i in range(2):
-            for o in range(4):
-                ybuf[step, i, o] = out[(4 * i + o) * 64 : (4 * i + o + 1) * 64]
-        for i in range(2):
-            here = jnp.logical_and(lax.rem(step, 4) == 2, col == i)
+            here = is_local(step, i)
 
             @pl.when(here)
             def _():
@@ -144,152 +208,7 @@
             def _(i=i):
                 y_copy(step, i).start()
 
-    loop(8, main)
-
-    def finish(step):
-        for i in range(2):
-            here = jnp.logical_and(lax.rem(step, 4) == 2, col == i)
-
-            @pl.when(here)
-            def _():
-                y_local(step // 4).wait()
-
-            @pl.when(jnp.logical_not(here))
-            def _(i=i):
-                y_copy(step, i).wait_send()
-
-        half = step // 4
-        src_x = lax.rem(step, 4)
-        for i in range(2):
-            @pl.when(jnp.logical_or(src_x != x, col != i))
-            def _(i=i):
-                dst = out_hbm.at[half, pl.ds(4 * src_x, 4), pl.ds(64 * i, 64)]
-                pltpu.make_async_remote_copy(ybuf.at[0, 0], dst, y_send.at[0], y_recv.at[half * 8 + 2 * src_x + i], device_id={"col": i, "row": base_row + src_x}, device_id_type=MESH).wait_recv()
-
-        @pl.when(row < row_size - 1)
-        def _():
-            halo_copy(step).wait_send()
-
-
-    loop(8, finish)
-
-    @pl.when(col == 0)
-    def _():
-        col_copy().wait_send()
-
-        @pl.when(row < row_size - 1)
-        def _():
-            corn_copy().wait_send()
-
-
-def down_one(row_size, images, w, b):
-    def kernel(*refs):
-        down_one_kernel(row_size, *refs)
-
-    return pl.pallas_call(
-        kernel,
-        out_shape=jax.ShapeDtypeStruct((2, 16, 128, 512), BF16),
-        in_specs=[ANY_SPEC, VM_SPEC, VM_SPEC],
-        out_specs=ANY_SPEC,
-        scratch_shapes=[
-            VM((2, 2, 8, 128, 256), BF16),
-            VM((8, 2, 128, 256), BF16),
-            VM((16, 8, 16, 256), BF16),
-            VM((16, 16, 256), BF16),
-            VM((2, 144, 128), F32),
-            VM((2, 9, 64, 768), BF16),
-            VM((8, 2, 4, 64, 512), BF16),
-            SEM((2,)),
-            SEM((8,)),
-            SEM((8,)),
-            SEM((2,)),
-            SEM((2,)),
-            SEM((16,)),
-            SEM((16,)),
-            SEM((2,)),
-        ],
-        compiler_params=PARAMS,
-        name="down_one",
-    )(images, w.reshape(3, 768, 512), b.reshape(1, 512))
-
-
-def shifted(value, by, width):
-    size = value.shape[0]
-    pos = lax.rem(lax.broadcasted_iota(jnp.int32, (size, 1), 0), width)
-    edge = 0 if by == 1 else width - 1
-    return jnp.where(pos == edge, 0.0, pltpu.roll(value, by % size, 0))
-
-
-def split_columns(value, scratch, even_ref, odd_ref, index, lane, rows, width):
-    half = width // 2
-    for h in range(2):
-        scratch[h] = value[:, 128 * h : 128 * h + 128]
-        lanes = pl.ds(pl.multiple_of(lane + 128 * h, 128), 128)
-        for ref, start in ((even_ref, 0), (odd_ref, 1)):
-            part = scratch[h, pl.ds(start, rows * half, stride=2)].astype(BF16)
-            ref[index[0], index[1], :, lanes] = part.reshape(rows, half, 128)
-
-
-def middle_kernel(row_size, y1_hbm, w1_hbm, w2_hbm, w3_hbm, b1_ref, b2_ref, b3_ref, even2, odd2, y1v, w1, w2, w3, even1, odd1, y2v, scratch, w_sem, in_sem, ha_s, ha_r, hb_s, hb_r, hc_s, hc_r, hd_s, hd_r):
-    row = lax.axis_index("row")
-    has_up = row >= 4
-    has_down = row < row_size - 4
-
-    def remote(src, dst, send, recv, delta):
-        return pltpu.make_async_remote_copy(src, dst, send, recv, device_id={"row": row + delta}, device_id_type=MESH)
-
-    def halo1_down(i):
-        return remote(y1_hbm.at[i, 15], y1v.at[i, 0], ha_s.at[i], ha_r.at[i], 4)
-
-    def halo1_up(i):
-        return remote(y1_hbm.at[i, 0], y1v.at[i, 17], ha_s.at[2 + i], ha_r.at[2 + i], -4)
-
-    def halo2(i, which):
-        ref = (even1, odd1)[which]
-        return remote(ref.at[i, 16], ref.at[i, 0], hb_s.at[2 * i + which], hb_r.at[2 * i + which], 4)
-
-    def halo3_down(i):
-        return remote(y2v.at[i, 8], y2v.at[i, 0], hc_s.at[i], hc_r.at[i], 4)
-
-    def halo3_up(i):
-        return remote(y2v.at[i, 1], y2v.at[i, 9], hc_s.at[2 + i], hc_r.at[2 + i], -4)
-
-    def halo4(i, which):
-        ref = (even2, odd2)[which]
-        return remote(ref.at[i, 8], ref.at[i, 0], hd_s.at[2 * i + which], hd_r.at[2 * i + which], 4)
-
-    loads = [pltpu.make_async_copy(y1_hbm.at[i], y1v.at[i, pl.ds(1, 16)], in_sem.at[i]) for i in range(2)]
-    weights = [pltpu.make_async_copy(src, dst, w_sem.at[n]) for n, (src, dst) in enumerate(((w1_hbm, w1), (w2_hbm, w2), (w3_hbm, w3)))]
-
-    @pl.when(has_down)
-    def _():
-        for i in range(2):
-            halo1_down(i).start()
-
-    @pl.when(has_up)
-    def _():
-        for i in range(2):
-            halo1_up(i).start()
-
-    weights[0].start()
-    for i in range(2):
-        loads[i].start()
-
-    @pl.when(jnp.logical_not(has_up))
-    def _():
-        for i in range(2):
-            for ref in (y1v, even1, odd1, y2v, even2, odd2):
-                ref[i, 0] = jnp.zeros(ref.shape[2:], BF16)
-
-    @pl.when(jnp.logical_not(has_down))
-    def _():
-        for i in range(2):
-            y1v[i, 17] = jnp.zeros(y1v.shape[2:], BF16)
-            y2v[i, 9] = jnp.zeros(y2v.shape[2:], BF16)
-
-    for i in range(2):
-        loads[i].wait()
-    weights[0].wait()
+    loop(8, stage_d1)
 
     def refine_block(src, i, first, rows, w, lanes):
         width = src.shape[2]
@@ -301,42 +220,37 @@
             parts.append(jnp.dot(lhs, rhs, preferred_element_type=F32))
         return parts[1] + shifted(parts[0], 1, width) + shifted(parts[2], -1, width)
 
-    def stage_r1(step):
-        i = lax.rem(step, 2)
-        block = lax.rem(1 + step // 2, 4)
-        for n in (1, 2):
-            @pl.when(step == n)
-            def _(n=n):
-                weights[n].start()
-
-        @pl.when(step == 4)
-        def _():
-            @pl.when(has_down)
+    def lanes_of(n):
+        return pl.ds(pl.multiple_of(n * 256, 256), 256)
+
+    def stage_r1(i):
+        def piece(step):
+            block = lax.rem(1 + step, 4)
+
+            @pl.when(block == 3)
             def _():
-                for k in range(2):
-                    halo1_up(k).wait_recv()
-
-            @pl.when(has_up)
+                @pl.when(has_down)
+                def _():
+                    halo1_up(i).wait_recv()
+
+                @pl.when(has_up)
+                def _():
+                    halo1_down(i).wait_recv()
+
+            def chunk(n):
+                lanes = lanes_of(n)
+                out = refine_block(y1v, i, 4 * block, 4, w1, lanes)
+                out = jnp.maximum(out + b1_ref[:, lanes], 0.0)
+                split_columns(out, scratch, even1, odd1, (i, pl.ds(1 + 4 * block, 4)), n * 256, 4, 128)
+
+            loop(2, chunk)
+
+            @pl.when(jnp.logical_and(has_down, block == 3))
             def _():
-                for k in range(2):
-                    halo1_down(k).wait_recv()
-
-        def chunk(n):
-            lanes = pl.ds(pl.multiple_of(n * 256, 256), 256)
-            out = refine_block(y1v, i, 4 * block, 4, w1, lanes)
-            out = jnp.maximum(out + b1_ref[:, lanes], 0.0)
-            split_columns(out, scratch, even1, odd1, (i, pl.ds(1 + 4 * block, 4)), n * 256, 4, 128)
-
-        loop(2, chunk)
-
-        @pl.when(jnp.logical_and(has_down, block == 3))
-        def _():
-            for which in range(2):
-                halo2(i, which).start()
-
-
-    loop(8, stage_r1)
-    weights[1].wait()
+                for which in range(2):
+                    halo2(i, which).start()
+
+        loop(4, piece)
 
     def stage_d2(i):
         @pl.when(has_up)
@@ -345,7 +259,7 @@
                 halo2(i, which).wait_recv()
 
         def chunk(n):
-            lanes = pl.ds(pl.multiple_of(n * 256, 256), 256)
+            lanes = lanes_of(n)
 
             def gather(ref):
                 return [jnp.concatenate([ref[i, 2 * o + dy] for o in range(8)], axis=0) for dy in range(3)]
@@ -369,11 +283,7 @@
         def _():
             halo3_up(i).start()
 
-
-    loop(2, stage_d2)
-    weights[2].wait()
-
-    def stage_r2(i):
+    def halo3_wait(i):
         @pl.when(has_up)
         def _():
             halo3_down(i).wait_recv()
@@ -382,21 +292,82 @@
         def _():
             halo3_up(i).wait_recv()
 
-        def chunk(n):
-            lanes = pl.ds(pl.multiple_of(n * 256, 256), 256)
+    def stage_r2(i, first, count):
+        def chunk(step):
+            n = first + step
+            lanes = lanes_of(n)
             out = refine_block(y2v, i, 0, 8, w3, lanes)
             out = jnp.maximum(out + b3_ref[:, lanes], 0.0)
             split_columns(out, scratch, even2, odd2, (i, pl.ds(1, 8)), n * 256, 8, 64)
 
-        loop(4, chunk)
-
+        loop(count, chunk)
+
+    def halo4_start(i):
         @pl.when(has_down)
         def _():
             for which in range(2):
                 halo4(i, which).start()
 
-
-    loop(2, stage_r2)
+    def per_image(half):
+        y_local(half).wait()
+        for xs in range(4):
+            for cs in range(2):
+                @pl.when(jnp.logical_or(xs != x, cs != col))
+                def _(xs=xs, cs=cs):
+                    pltpu.make_async_remote_copy(ybuf.at[0, 0], y_place(half, xs, cs), y_send.at[0], y_recv.at[half * 8 + 2 * xs + cs], device_id={"col": cs, "row": base_row + xs}, device_id_type=MESH).wait_recv()
+
+        @pl.when(has_down)
+        def _():
+            halo1_down(half).start()
+
+        @pl.when(has_up)
+        def _():
+            halo1_up(half).start()
+
+        @pl.when(half == 0)
+        def _():
+            weights[0].wait()
+
+        stage_r1(half)
+
+        @pl.when(half == 0)
+        def _():
+            weights[1].wait()
+
+        stage_d2(half)
+
+        @pl.when(half == 0)
+        def _():
+            halo3_wait(0)
+            weights[2].wait()
+
+        stage_r2(0, 2 * half, 2)
+
+    loop(2, per_image)
+    halo4_start(0)
+    halo3_wait(1)
+    stage_r2(1, 0, 4)
+    halo4_start(1)
+
+    def finish(step):
+        for i in range(2):
+            @pl.when(jnp.logical_not(is_local(step, i)))
+            def _(i=i):
+                y_copy(step, i).wait_send()
+
+        @pl.when(sends_row)
+        def _():
+            halo_copy(step).wait_send()
+
+    loop(8, finish)
+
+    @pl.when(col == 0)
+    def _():
+        col_copy().wait_send()
+
+        @pl.when(sends_row)
+        def _():
+            corn_copy().wait_send()
 
     @pl.when(has_down)
     def _():
@@ -416,16 +387,23 @@
                 halo4(i, which).wait_recv()
 
 
-def middle(row_size, y1, w1, w2, w3, b1, b2, b3):
+def front(row_size, images, w0, b0, w1, w2, w3, b1, b2, b3):
     def kernel(*refs):
-        middle_kernel(row_size, *refs)
+        front_kernel(row_size, *refs)
 
     return pl.pallas_call(
         kernel,
         out_shape=[jax.ShapeDtypeStruct((2, 9, 32, 1024), BF16)] * 2,
-        in_specs=[ANY_SPEC] * 4 + [VM_SPEC] * 3,
+        in_specs=[ANY_SPEC, VM_SPEC, VM_SPEC] + [ANY_SPEC] * 3 + [VM_SPEC] * 3,
         out_specs=[VM_SPEC] * 2,
         scratch_shapes=[
+            VM((2, 2, 8, 128, 256), BF16),
+            VM((8, 2, 128, 256), BF16),
+            VM((16, 8, 16, 256), BF16),
+            VM((16, 16, 256), BF16),
+            VM((2, 144, 128), F32),
+            VM((2, 9, 64, 768), BF16),
+            VM((8, 2, 4, 64, 512), BF16),
             VM((2, 18, 128, 512), BF16),
             VM((3, 3, 512, 512), BF16),
             VM((3, 3, 512, 1024), BF16),
@@ -434,13 +412,12 @@
             VM((2, 17, 64, 512), BF16),
             VM((2, 10, 64, 1024), BF16),
             VM((2, 512, 128), F32),
-            SEM((3,)),
-            SEM((2,)),
         ]
+        + [SEM((n,)) for n in (2, 8, 8, 2, 2, 16, 16, 2, 3)]
         + [SEM((4,))] * 8,
         compiler_params=PARAMS,
-        name="middle",
-    )(y1, w1, w2, w3, b1.reshape(1, -1), b2.reshape(1, -1), b3.reshape(1, -1))
+        name="front",
+    )(images, w0.reshape(3, 768, 512), b0.reshape(1, 512), w1, w2, w3, b1.reshape(1, -1), b2.reshape(1, -1), b3.reshape(1, -1))
 
 
 RING = 4
@@ -629,8 +606,7 @@
     row_size = mesh.shape["row"]
 
     def local_encoder(images, w_down1, b_down1, w_refine1, b_refine1, w_down2, b_down2, w_refine2, b_refine2, w_down3, b_down3, w_refine3, b_refine3):
-        y = down_one(row_size, images, w_down1, b_down1)
-        even, odd = middle(row_size, y, w_refine1, w_down2, w_refine2, b_refine1, b_down2, b_refine2)
+        even, odd = front(row_size, images, w_down1, b_down1, w_refine1, w_down2, w_refine2, b_refine1, b_down2, b_refine2)
         out = last(row_size, even, odd, w_down3, w_refine3, b_down3, b_refine3)
         return out.reshape(16, 1, 16, 2048)
 

time: 220 us -> 203 us (0.923)
  Pallas kernels: 218 us -> 201 us
    pallas_call x2 -> x1, Pallas kernels: 157 us -> 140 us  [front(): pl.pallas_call(kernel, out_shape=[jax.ShapeDtypeStruct((2, 9, 32, 1024),...]
where the time goes in v1:
time: 203 us
  Pallas kernels  201 us (99%)
  local copies, waits for them, and re-layouts  2.3 us (1%)
    pallas_call x1, Pallas kernels, front(): pl.pallas_call(kernel, out_shape=[jax.ShapeDtypeStruct((2, 9, 32, 1024),...  140 us
    pallas_call x1, Pallas kernels, last(): pl.pallas_call(kernel, out_shape=jax.ShapeDtypeStruct((4, 2, 2, 16, 2048)...  60.5 us

profile of v1, /device:TPU:1, one launch (start us, length us, event | category | flops | bytes accessed | tf_op | source)
XLA Modules:
  0.0 202.8 jit_solution(3995896539648679668)
XLA Ops:
  0.0 140.0 %front.1 = (bf16[2,9,32,1024]{3,2,1,0:T(8,128)(2,1)}, bf16[2,9,32,1024]{3,2,1,0:T(8,128)(2,1)}) custom-call(bf16[16,8,128,256]{3,2,1,0:T(8,128)(2,1)} %refs_0_.1, bf16[3,768,512]{2,1,0:T(8,128)(2,1)} %bitcast.11, f32[1,512]{1,0:T(1,128)} %bitcast.16, bf16[3,3,512,512]{3,2,1,0:T(8,128)(2,1)} %refs_3_.2, bf16[3,3,512,1024]{3,2,1,0:T(8,128)(2,1)} %refs_4_.1, ...), custom_call_target="tpu_custom_call" | custom-call | tf_op jit(solution)/shard_map/front/pallas_call | solution.py:394
  140.0 60.5 %last.1 = bf16[4,2,2,16,2048]{4,3,2,1,0:T(8,128)(2,1)} custom-call(bf16[2,9,32,1024]{3,2,1,0:T(8,128)(2,1)} %get-tuple-element.7.refs_0_, bf16[2,9,32,1024]{3,2,1,0:T(8,128)(2,1)} %get-tuple-element.8.refs_1_, bf16[3,3,1024,2048]{3,2,1,0:T(8,128)(2,1)} %refs_2_.1, bf16[3,3,2048,2048]{3,2,1,0:T(8,128)(2,1)} %refs_3_.3, f32[1,2048]{1,0:T(1,128)} %bitcast.12, ...), custom_call_target="tpu_custom_call" | custom-call | tf_op jit(solution)/shard_map/last/pallas_call | solution.py:584
  200.5 2.3 %copy.16 = bf16[16,1,16,2048]{3,2,1,0:T(8,128)(2,1)} copy(bf16[16,1,16,2048]{3,2,1,0:T(8,128)(2,1)} %bitcast.10) | data formatting | bytes 2097152

commit v2 on v1

v2 whole, which is shorter than its diff:
```python
import jax
import jax.numpy as jnp
from jax import lax
from jax.experimental import pallas as pl
from jax.experimental.pallas import tpu as pltpu
from jax.sharding import PartitionSpec as P

MESH = pl.DeviceIdType.MESH
BF16 = jnp.bfloat16
F32 = jnp.float32
WIDE = 512
TOP = 2048
MID = 1024
PART = 256
LANE = 128
HALF = 64
VM = pltpu.VMEM
SEM = pltpu.SemaphoreType.DMA
ANY_SPEC = pl.BlockSpec(memory_space=pl.ANY)
VM_SPEC = pl.BlockSpec(memory_space=VM)
PARAMS = pltpu.CompilerParams(has_side_effects=True, vmem_limit_bytes=67043328)


def loop(count, fn):
    def body(step, carry):
        fn(step)
        return carry

    lax.fori_loop(0, count, body, 0)


def shifted(value, by, width):
    size = value.shape[0]
    pos = lax.rem(lax.broadcasted_iota(jnp.int32, (size, 1), 0), width)
    edge = 0 if by == 1 else width - 1
    return jnp.where(pos == edge, 0.0, pltpu.roll(value, by % size, 0))


def split_columns(value, scratch, even_ref, odd_ref, index, lane, rows, width):
    half = width // 2
    for h in range(2):
        scratch[h, 0 : rows * width] = value[:, LANE * h : LANE * h + LANE]
        lanes = pl.ds(pl.multiple_of(lane + LANE * h, LANE), LANE)
        for ref, start in ((even_ref, 0), (odd_ref, 1)):
            part = scratch[h, pl.ds(start, rows * half, stride=2)].astype(BF16)
            ref[index[0], index[1], :, lanes] = part.reshape(rows, half, LANE)


def encoder_kernel(row_size, img_hbm, w0_ref, b0_ref, w1_hbm, w2_hbm, w3_hbm, w4_hbm, w5_hbm, b1_ref, b2_ref, b3_ref, b4_ref, b5_ref, out_hbm, inb, halo, colb, corn, frow, xbuf, ybuf, y1v, wbuf, eo1, y2v, scratch, eo2, y3v, acc, in_sem, halo_send, halo_recv, col_sem, corn_sem, y_send, y_recv, self_sem, w_sem, ha_s, ha_r, hb_s, hb_r, hc_s, hc_r, hd_s, hd_r, up_s, up_r, down_s, down_r, out_sem, w4_sem, w5_sem, o_s, o_r):
    col = lax.axis_index("col")
    row = lax.axis_index("row")
    x = lax.rem(row, 4)
    base_row = row - x
    has_up = row >= 4
    has_down = row < row_size - 4
    sends_row = row < row_size - 1
    total = 3 * (TOP // WIDE)

    def plane(src, part, first, count, n):
        return pltpu.make_async_copy(src.at[:, :, pl.ds(WIDE * part, WIDE)], wbuf.at[pl.ds(first, count)], w_sem.at[n])

    weights = [[plane(w1_hbm, 0, 0, 9, 0)], [plane(w2_hbm, k, 9 + 9 * k, 9, 1 + k) for k in range(2)], [plane(w3_hbm, k, 27 + 18 * k, 18, 3 + k) for k in range(2)]]

    def weights_start(n):
        for copy in weights[n]:
            copy.start()

    def weights_wait(n):
        for copy in weights[n]:
            copy.wait()

    def wide(n):
        return pl.ds(pl.multiple_of(n * WIDE, WIDE), WIDE)

    def load4(t):
        slot = lax.rem(t, 4)
        return [pltpu.make_async_copy(w4_hbm.at[dy, lax.rem(t + 1, 3), :, :, wide(t // 3)], wbuf.at[pl.ds(6 * slot + 2 * dy, 2)], w4_sem.at[slot, dy]) for dy in range(3)]

    def base5(t):
        return lax.rem(27 + 12 * lax.rem(t, 5), 63)

    def load5(t):
        return [pltpu.make_async_copy(w5_hbm.at[dy, lax.rem(t + 1, 3), :, :, wide(t // 3)], wbuf.at[pl.ds(base5(t) + 4 * dy, 4)], w5_sem.at[lax.rem(t, 5), dy]) for dy in range(3)]

    def start_all(copies):
        for copy in copies:
            copy.start()

    def wait_all(copies):
        for copy in copies:
            copy.wait()

    def group_of(step, xpos):
        turn = lax.rem(step, 4)
        turn = jnp.where(turn < 2, turn + col * (1 - 2 * turn), turn)
        return lax.rem(xpos + 6 - turn, 4)

    def image_of(step, xpos):
        return 4 * group_of(step, xpos) + 2 * (step // 4)

    def load(step):
        slot = lax.rem(step, 2)
        return pltpu.make_async_copy(img_hbm.at[pl.ds(image_of(step, x), 2)], inb.at[slot], in_sem.at[slot])

    def halo_copy(step):
        first = image_of(step, lax.rem(x + 1, 4))
        return pltpu.make_async_remote_copy(img_hbm.at[pl.ds(first, 2), 7], halo.at[step], halo_send.at[step], halo_recv.at[step], device_id={"row": row + 1}, device_id_type=MESH)

    def col_copy():
        return pltpu.make_async_remote_copy(img_hbm.at[:, :, pl.ds(120, 8)], colb, col_sem.at[0], col_sem.at[1], device_id={"col": 1}, device_id_type=MESH)

    def corn_copy():
        return pltpu.make_async_remote_copy(img_hbm.at[:, 7, pl.ds(120, 8)], corn, corn_sem.at[0], corn_sem.at[1], device_id={"col": 1, "row": row + 1}, device_id_type=MESH)

    def y_place(half, xs, cs):
        return y1v.at[half, pl.ds(1 + 4 * xs, 4), pl.ds(pl.multiple_of(HALF * cs, HALF), HALF)]

    def y_copy(step, i):
        half = step // 4
        return pltpu.make_async_remote_copy(ybuf.at[step, i], y_place(half, x, col), y_send.at[step * 2 + i], y_recv.at[half * 8 + 2 * x + col], device_id={"col": i, "row": base_row + group_of(step, x)}, device_id_type=MESH)

    def y_local(half):
        return pltpu.make_async_copy(ybuf.at[4 * half + 2, col], y_place(half, x, col), self_sem.at[half])

    def ring(src, dst, send, recv, delta):
        return pltpu.make_async_remote_copy(src, dst, send, recv, device_id={"row": row + delta}, device_id_type=MESH)

    def halo1_down(i):
        return ring(y1v.at[i, 16], y1v.at[i, 0], ha_s.at[i], ha_r.at[i], 4)

    def halo1_up(i):
        return ring(y1v.at[i, 1], y1v.at[i, 17], ha_s.at[2 + i], ha_r.at[2 + i], -4)

    def halo2(i):
        return ring(eo1.at[:, i, 16], eo1.at[:, i, 0], hb_s.at[i], hb_r.at[i], 4)

    def halo3_down(i):
        return ring(y2v.at[i, 8], y2v.at[i, 0], hc_s.at[i], hc_r.at[i], 4)

    def halo3_up(i):
        return ring(y2v.at[i, 1], y2v.at[i, 9], hc_s.at[2 + i], hc_r.at[2 + i], -4)

    def halo4(i):
        return ring(eo2.at[:, i, 8], eo2.at[:, i, 0], hd_s.at[i], hd_r.at[i], 4)

    load(0).start()

    @pl.when(col == 0)
    def _():
        col_copy().start()

    @pl.when(sends_row)
    def _():
        @pl.when(col == 0)
        def _():
            corn_copy().start()

        def body(step):
            halo_copy(step).start()

        loop(8, body)

    @pl.when(col == 0)
    def _():
        colb[...] = jnp.zeros_like(colb)

    @pl.when(jnp.logical_or(col == 0, row == 0))
    def _():
        corn[...] = jnp.zeros_like(corn)

    @pl.when(row == 0)
    def _():
        halo[...] = jnp.zeros_like(halo)

    @pl.when(jnp.logical_not(has_up))
    def _():
        for i in range(2):
            for ref in (y1v, y2v):
                ref[i, 0] = jnp.zeros(ref.shape[2:], BF16)
            for ref in (eo1, eo2):
                ref[:, i, 0] = jnp.zeros((2,) + ref.shape[3:], BF16)
        y3v[:, 0] = jnp.zeros((2, 32, TOP), BF16)

    @pl.when(jnp.logical_not(has_down))
    def _():
        for i in range(2):
            y1v[i, 17] = jnp.zeros(y1v.shape[2:], BF16)
            y2v[i, 9] = jnp.zeros(y2v.shape[2:], BF16)
        y3v[:, 5] = jnp.zeros((2, 32, TOP), BF16)

    @pl.when(col == 1)
    def _():
        col_copy().wait_recv()

        @pl.when(row > 0)
        def _():
            corn_copy().wait_recv()

    def taps(i, q, left, line):
        for h in range(2):
            lanes = slice(LANE * h, LANE * h + LANE)
            frow[h, 0:8] = left[:, lanes].astype(F32)
            frow[h, 8:136] = line[:, lanes].astype(F32)
        for t in range(3):
            for h in range(2):
                xbuf[i, q, :, PART * t + LANE * h : PART * t + LANE * h + LANE] = frow[h, pl.ds(7 + t, HALF, stride=2)].astype(BF16)

    def is_local(step, i):
        return jnp.logical_and(lax.rem(step, 4) == 2, col == i)

    def stage_d1(step):
        slot = lax.rem(step, 2)
        first = image_of(step, x)

        @pl.when(step < 7)
        def _():
            load(step + 1).start()

        for n in range(3):
            @pl.when(step == n + 1)
            def _(n=n):
                weights_start(n)

        load(step).wait()

        @pl.when(row > 0)
        def _():
            halo_copy(step).wait_recv()

        for i in range(2):
            taps(i, 0, corn[first + i], halo[step, i])

            def line(q, i=i):
                taps(i, q + 1, colb[first + i, q], inb[slot, i, q])

            loop(8, line)
        acc = None
        for dy in range(3):
            lhs = jnp.concatenate([xbuf[i, 2 * o + dy] for i in range(2) for o in range(4)], axis=0)
            part = jnp.dot(lhs, w0_ref[dy], preferred_element_type=F32)
            acc = part if acc is None else acc + part
        out = jnp.maximum(acc + b0_ref[...], 0.0).astype(BF16)
        ybuf[step] = out.reshape(2, 4, HALF, WIDE)
        for i in range(2):
            here = is_local(step, i)

            @pl.when(here)
            def _():
                y_local(step // 4).start()

            @pl.when(jnp.logical_not(here))
            def _(i=i):
                y_copy(step, i).start()

    loop(8, stage_d1)

    def tap(base, size, dy, dx, n):
        first = base + (n // 2) * 9 * size + (3 * dy + dx) * size
        return wbuf[pl.ds(first, size), :, lanes_of(lax.rem(n, 2))].reshape(WIDE * size, PART)

    def refine_block(src, i, first, rows, base, size, n):
        width = src.shape[2]
        m = rows * width
        lhs = jnp.concatenate([src[i, pl.ds(first + dy, rows)].reshape(m, -1) for dy in range(3)], axis=1)
        parts = []
        for dx in range(3):
            rhs = jnp.concatenate([tap(base, size, dy, dx, n) for dy in range(3)], axis=0)
            parts.append(jnp.dot(lhs, rhs, preferred_element_type=F32))
        return parts[1] + shifted(parts[0], 1, width) + shifted(parts[2], -1, width)

    def lanes_of(n):
        return pl.ds(pl.multiple_of(n * PART, PART), PART)

    def stage_r1(i):
        def piece(step):
            block = lax.rem(1 + step, 4)

            @pl.when(block == 3)
            def _():
                @pl.when(has_down)
                def _():
                    halo1_up(i).wait_recv()

                @pl.when(has_up)
                def _():
                    halo1_down(i).wait_recv()

            def chunk(n):
                lanes = lanes_of(n)
                out = refine_block(y1v, i, 4 * block, 4, 0, 1, n)
                out = jnp.maximum(out + b1_ref[:, lanes], 0.0)
                split_columns(out, scratch, eo1.at[0], eo1.at[1], (i, pl.ds(1 + 4 * block, 4)), n * PART, 4, LANE)

            loop(2, chunk)

            @pl.when(jnp.logical_and(has_down, block == 3))
            def _():
                halo2(i).start()

        loop(4, piece)

    def stage_d2(i):
        @pl.when(has_up)
        def _():
            halo2(i).wait_recv()

        def chunk(n):
            lanes = lanes_of(n)

            def gather(ref):
                return [jnp.concatenate([eo1[ref, i, 2 * o + dy] for o in range(8)], axis=0) for dy in range(3)]

            odd = gather(1)
            both = jnp.concatenate(gather(0) + odd, axis=1)
            rhs = jnp.concatenate([tap(9, 1, dy, dx, n) for dx in (1, 2) for dy in range(3)], axis=0)
            left = jnp.concatenate([tap(9, 1, dy, 0, n) for dy in range(3)], axis=0)
            out = jnp.dot(both, rhs, preferred_element_type=F32)
            out = out + shifted(jnp.dot(jnp.concatenate(odd, axis=1), left, preferred_element_type=F32), 1, HALF)
            out = jnp.maximum(out + b2_ref[:, lanes], 0.0).astype(BF16)
            y2v[i, 1:9, :, lanes] = out.reshape(8, HALF, PART)

        loop(4, chunk)

        @pl.when(has_down)
        def _():
            halo3_down(i).start()

        @pl.when(has_up)
        def _():
            halo3_up(i).start()

    def halo3_wait(i):
        @pl.when(has_up)
        def _():
            halo3_down(i).wait_recv()

        @pl.when(has_down)
        def _():
            halo3_up(i).wait_recv()

    def stage_r2(i, begin, count, top, rows):
        def chunk(step):
            n = begin + step
            lanes = lanes_of(n)
            out = refine_block(y2v, i, top, rows, 27, 2, n)
            out = jnp.maximum(out + b3_ref[:, lanes], 0.0)
            split_columns(out, scratch, eo2.at[0], eo2.at[1], (i, pl.ds(1 + top, rows)), n * PART, rows, HALF)

        loop(count, chunk)

    def halo4_start(i):
        @pl.when(has_down)
        def _():
            halo4(i).start()

    def per_image(half):
        y_local(half).wait()
        for xs in range(4):
            for cs in range(2):
                @pl.when(jnp.logical_or(xs != x, cs != col))
                def _(xs=xs, cs=cs):
                    pltpu.make_async_remote_copy(ybuf.at[0, 0], y_place(half, xs, cs), y_send.at[0], y_recv.at[half * 8 + 2 * xs + cs], device_id={"col": cs, "row": base_row + xs}, device_id_type=MESH).wait_recv()

        @pl.when(has_down)
        def _():
            halo1_down(half).start()

        @pl.when(has_up)
        def _():
            halo1_up(half).start()

        @pl.when(half == 0)
        def _():
            weights_wait(0)

        stage_r1(half)

        @pl.when(half == 0)
        def _():
            weights_wait(1)

        stage_d2(half)

        @pl.when(half == 0)
        def _():
            halo3_wait(0)
            weights_wait(2)

        @pl.when(half == 1)
        def _():
            for t in range(4):
                start_all(load4(t))

        stage_r2(0, 2 * half, 2, 0, 8)

    loop(2, per_image)
    halo4_start(0)
    halo3_wait(1)
    stage_r2(1, 0, 4, 4, 4)
    halo4_start(1)
    stage_r2(1, 0, 4, 0, 4)

    @pl.when(has_up)
    def _():
        for i in range(2):
            halo4(i).wait_recv()

    def halo_up(n):
        return pltpu.make_async_remote_copy(y3v.at[:, 1, :, wide(n)], y3v.at[:, 5, :, wide(n)], up_s.at[n], up_r.at[n], device_id={"row": row - 4}, device_id_type=MESH)

    def halo_down(n):
        return pltpu.make_async_remote_copy(y3v.at[:, 4, :, wide(n)], y3v.at[:, 0, :, wide(n)], down_s.at[n], down_r.at[n], device_id={"row": row + 4}, device_id_type=MESH)

    def out_copy(n, xd, cd):
        dst = out_hbm.at[x, :, col, :, wide(n)]
        return pltpu.make_async_remote_copy(ybuf.at[n, :, xd, pl.ds(16 * cd, 16)], dst, o_s.at[n, 2 * xd + cd], o_r.at[n, 2 * x + col], device_id={"col": cd, "row": base_row + xd}, device_id_type=MESH)

    def out_recv(n, xs, cs):
        dst = out_hbm.at[xs, :, cs, :, wide(n)]
        return pltpu.make_async_remote_copy(ybuf.at[n, :, xs, pl.ds(16 * cs, 16)], dst, o_s.at[n, 2 * xs + cs], o_r.at[n, 2 * xs + cs], device_id={"col": cs, "row": base_row + xs}, device_id_type=MESH)

    def out_self(n):
        dst = out_hbm.at[x, :, col, :, wide(n)]
        return pltpu.make_async_copy(ybuf.at[n, :, x, pl.ds(pl.multiple_of(16 * col, 16), 16)], dst, out_sem.at[n])

    def stage_d3(t):
        wait_all(load4(t))
        ahead = t + 3

        @pl.when(jnp.logical_and(t >= 1, ahead < total))
        def _():
            start_all(load4(ahead))

        for k in range(3):
            @pl.when(t == 3 + 2 * k)
            def _(k=k):
                start_all(load5(k))

        j = lax.rem(t, 3)
        n = t // 3
        plane_index = (j + 1) // 2
        lhs = jnp.concatenate([jnp.concatenate([eo2[plane_index, i, 2 * o + dy] for i in range(2) for o in range(4)], axis=0) for dy in range(3)], axis=1)
        rhs = wbuf[pl.ds(6 * lax.rem(t, 4), 6)].reshape(3072, WIDE)
        acc[j] = jnp.dot(lhs, rhs, preferred_element_type=F32)

        @pl.when(j == 2)
        def _():
            out = acc[0] + acc[1] + shifted(acc[2], 1, 32)
            out = jnp.maximum(out + b4_ref[:, wide(n)], 0.0).astype(BF16)
            y3v[:, 1:5, :, wide(n)] = out.reshape(2, 4, 32, WIDE)

            @pl.when(has_up)
            def _():
                halo_up(n).start()

            @pl.when(has_down)
            def _():
                halo_down(n).start()

    loop(total, stage_d3)
    for t in (3, 4):
        start_all(load5(t))

    def finish(step):
        for i in range(2):
            @pl.when(jnp.logical_not(is_local(step, i)))
            def _(i=i):
                y_copy(step, i).wait_send()

        @pl.when(sends_row)
        def _():
            halo_copy(step).wait_send()

    loop(8, finish)

    def halo_wait(n):
        @pl.when(has_down)
        def _():
            halo_up(n).wait_recv()

        @pl.when(has_up)
        def _():
            halo_down(n).wait_recv()

    loop(total // 3, halo_wait)

    def stage_r3(t):
        wait_all(load5(t))
        ahead = t + 4

        @pl.when(jnp.logical_and(t >= 1, ahead < total))
        def _():
            start_all(load5(ahead))

        j = lax.rem(t, 3)
        n = t // 3
        lhs = jnp.concatenate([y3v[:, dy : dy + 4].reshape(PART, TOP) for dy in range(3)], axis=1)
        rhs = wbuf[pl.ds(base5(t), 12)].reshape(6144, WIDE)
        acc[j] = jnp.dot(lhs, rhs, preferred_element_type=F32)

        @pl.when(j == 2)
        def _():
            out = acc[0] + shifted(acc[1], -1, 32) + shifted(acc[2], 1, 32)
            out = jnp.maximum(out + b5_ref[:, wide(n)], 0.0).astype(BF16)
            ybuf[n, :, :, 0:32] = out.reshape(2, 4, 32, WIDE)
            for xd in range(4):
                for cd in range(2):
                    here = jnp.logical_and(x == xd, col == cd)

                    @pl.when(here)
                    def _():
                        out_self(n).start()

                    @pl.when(jnp.logical_not(here))
                    def _(xd=xd, cd=cd):
                        out_copy(n, xd, cd).start()

    loop(total, stage_r3)

    def finish_out(n):
        out_self(n).wait()
        for xd in range(4):
            for cd in range(2):
                @pl.when(jnp.logical_or(x != xd, col != cd))
                def _(xd=xd, cd=cd):
                    out_copy(n, xd, cd).wait_send()
                    out_recv(n, xd, cd).wait_recv()

        @pl.when(has_up)
        def _():
            halo_up(n).wait_send()

        @pl.when(has_down)
        def _():
            halo_down(n).wait_send()

    loop(total // 3, finish_out)


    @pl.when(col == 0)
    def _():
        col_copy().wait_send()

        @pl.when(sends_row)
        def _():
            corn_copy().wait_send()

    @pl.when(has_down)
    def _():
        for i in range(2):
            halo1_down(i).wait_send()
            halo3_down(i).wait_send()
            halo2(i).wait_send()
            halo4(i).wait_send()

    @pl.when(has_up)
    def _():
        for i in range(2):
            halo1_up(i).wait_send()
            halo3_up(i).wait_send()


def encoder(row_size, images, weights, biases):
    def kernel(*refs):
        encoder_kernel(row_size, *refs)

    w0, w1, w2, w3, w4, w5 = weights
    flat = [b.reshape(1, -1) for b in biases]
    return pl.pallas_call(
        kernel,
        out_shape=jax.ShapeDtypeStruct((4, 2, 2, 16, TOP), BF16),
        in_specs=[ANY_SPEC, VM_SPEC, VM_SPEC] + [ANY_SPEC] * 5 + [VM_SPEC] * 5,
        out_specs=ANY_SPEC,
        scratch_shapes=[
            VM((2, 2, 8, LANE, PART), BF16),
            VM((8, 2, LANE, PART), BF16),
            VM((16, 8, 8, PART), BF16),
            VM((16, 8, PART), BF16),
            VM((2, 136, LANE), F32),
            VM((2, 9, HALF, 768), BF16),
            VM((8, 2, 4, HALF, WIDE), BF16),
            VM((2, 18, LANE, WIDE), BF16),
            VM((63, WIDE, WIDE), BF16),
            VM((2, 2, 17, HALF, WIDE), BF16),
            VM((2, 10, HALF, MID), BF16),
            VM((2, WIDE, LANE), F32),
            VM((2, 2, 9, 32, MID), BF16),
            VM((2, 6, 32, TOP), BF16),
            VM((3, PART, WIDE), F32),
        ]
        + [SEM((n,)) for n in (2, 8, 8, 2, 2, 16, 16, 2, 5)]
        + [SEM((4,))] * 13
        + [SEM(n) for n in ((4, 3), (5, 3), (4, 8), (4, 8))],
        compiler_params=PARAMS,
        name="encoder",
    )(images, w0.reshape(3, 768, WIDE), flat[0], w1.reshape(9, WIDE, WIDE), w2.reshape(9, WIDE, MID), w3.reshape(18, WIDE, MID), w4.reshape(3, 3, 2, WIDE, TOP), w5.reshape(3, 3, 4, WIDE, TOP), *flat[1:])


def solution(mesh):
    row_size = mesh.shape["row"]

    def local_encoder(images, w_down1, b_down1, w_refine1, b_refine1, w_down2, b_down2, w_refine2, b_refine2, w_down3, b_down3, w_refine3, b_refine3):
        weights = (w_down1, w_refine1, w_down2, w_refine2, w_down3, w_refine3)
        biases = (b_down1, b_refine1, b_down2, b_refine2, b_down3, b_refine3)
        return encoder(row_size, images, weights, biases).reshape(16, 1, 16, TOP)

    tile_spec = P("dp", "row", "col")
    return jax.shard_map(local_encoder, mesh=mesh, in_specs=(tile_spec,) + (P(),) * 12, out_specs=tile_spec, check_vma=False)
```

time: 203 us -> 176 us (0.87); the launches traced: 203 us -> 173 us
  Pallas kernels: 201 us -> 171 us
    pallas_call x2 -> x1, Pallas kernels: 201 us -> 171 us  [encoder(): pl.pallas_call(kernel, out_shape=jax.ShapeDtypeStruct((4, 2, 2, 16, TOP),...]
where the time goes in v2:
time: 176 us; the launch traced here: 173 us
  Pallas kernels  171 us (97%)
  local copies, waits for them, and re-layouts  2.3 us (1%)
    pallas_call x1, Pallas kernels, encoder(): pl.pallas_call(kernel, out_shape=jax.ShapeDtypeStruct((4, 2, 2, 16, TOP),...  171 us

profile of v2, /device:TPU:1, one launch (start us, length us, event | category | flops | bytes accessed | tf_op | source)
XLA Modules:
  0.0 173.5 jit_solution(17918174786041547655)
XLA Ops:
  0.0 171.2 %encoder.1 = bf16[4,2,2,16,2048]{4,3,2,1,0:T(8,128)(2,1)} custom-call(bf16[16,8,128,256]{3,2,1,0:T(8,128)(2,1)} %refs_0_.1, bf16[3,768,512]{2,1,0:T(8,128)(2,1)} %bitcast.20, f32[1,512]{1,0:T(1,128)} %bitcast.25, bf16[9,512,512]{2,1,0:T(8,128)(2,1)} %bitcast.18, bf16[9,512,1024]{2,1,0:T(8,128)(2,1)} %bitcast.17, bf16[18,512,1024]{2,1,0:T(8,128)(2,1)} %bitcast.16, ...), custom_call_target="tpu_custom_call" | custom-call | tf_op jit(solution)/shard_map/encoder/pallas_call | solution.py:569
  171.2 2.3 %copy.16 = bf16[16,1,16,2048]{3,2,1,0:T(8,128)(2,1)} copy(bf16[16,1,16,2048]{3,2,1,0:T(8,128)(2,1)} %bitcast.19) | data formatting | bytes 2097152

commit v3 on v2

--- a/solution.py
+++ b/solution.py
@@ -46,7 +46,7 @@
             ref[index[0], index[1], :, lanes] = part.reshape(rows, half, LANE)
 
 
-def encoder_kernel(row_size, img_hbm, w0_ref, b0_ref, w1_hbm, w2_hbm, w3_hbm, w4_hbm, w5_hbm, b1_ref, b2_ref, b3_ref, b4_ref, b5_ref, out_hbm, inb, halo, colb, corn, frow, xbuf, ybuf, y1v, wbuf, eo1, y2v, scratch, eo2, y3v, acc, in_sem, halo_send, halo_recv, col_sem, corn_sem, y_send, y_recv, self_sem, w_sem, ha_s, ha_r, hb_s, hb_r, hc_s, hc_r, hd_s, hd_r, up_s, up_r, down_s, down_r, out_sem, w4_sem, w5_sem, o_s, o_r):
+def encoder_kernel(row_size, img_hbm, w0_hbm, b0_ref, w1_hbm, w2_hbm, w3_hbm, w4_hbm, w5_hbm, b1_ref, b2_ref, b3_ref, b4_ref, b5_ref, out_hbm, inb, halo, colb, corn, frow, xbuf, ybuf, y1v, wbuf, eo1, y2v, scratch, eo2, y3v, acc, in_sem, halo_send, halo_recv, col_sem, corn_sem, y_send, y_recv, self_sem, w_sem, ha_s, ha_r, hb_s, hb_r, hc_s, hc_r, hd_s, hd_r, up_s, up_r, down_s, down_r, out_sem, w4_sem, w5_sem, o_s, o_r):
     col = lax.axis_index("col")
     row = lax.axis_index("row")
     x = lax.rem(row, 4)
@@ -61,6 +61,8 @@
 
     weights = [[plane(w1_hbm, 0, 0, 9, 0)], [plane(w2_hbm, k, 9 + 9 * k, 9, 1 + k) for k in range(2)], [plane(w3_hbm, k, 27 + 18 * k, 18, 3 + k) for k in range(2)]]
 
+    first_copy = pltpu.make_async_copy(w0_hbm, wbuf.at[pl.ds(27, 9), pl.ds(0, PART)], w_sem.at[5])
+
     def weights_start(n):
         for copy in weights[n]:
             copy.start()
@@ -143,6 +145,7 @@
     def halo4(i):
         return ring(eo2.at[:, i, 8], eo2.at[:, i, 0], hd_s.at[i], hd_r.at[i], 4)
 
+    first_copy.start()
     load(0).start()
 
     @pl.when(col == 0)
@@ -216,7 +219,7 @@
         def _():
             load(step + 1).start()
 
-        for n in range(3):
+        for n in range(2):
             @pl.when(step == n + 1)
             def _(n=n):
                 weights_start(n)
@@ -237,7 +240,8 @@
         acc = None
         for dy in range(3):
             lhs = jnp.concatenate([xbuf[i, 2 * o + dy] for i in range(2) for o in range(4)], axis=0)
-            part = jnp.dot(lhs, w0_ref[dy], preferred_element_type=F32)
+            rhs = wbuf[27 + 3 * dy : 30 + 3 * dy, 0:PART].reshape(768, WIDE)
+            part = jnp.dot(lhs, rhs, preferred_element_type=F32)
             acc = part if acc is None else acc + part
         out = jnp.maximum(acc + b0_ref[...], 0.0).astype(BF16)
         ybuf[step] = out.reshape(2, 4, HALF, WIDE)
@@ -252,7 +256,9 @@
             def _(i=i):
                 y_copy(step, i).start()
 
+    first_copy.wait()
     loop(8, stage_d1)
+    weights_start(2)
 
     def tap(base, size, dy, dx, n):
         first = base + (n // 2) * 9 * size + (3 * dy + dx) * size
@@ -381,19 +387,16 @@
 
         stage_d2(half)
 
-        @pl.when(half == 0)
-        def _():
-            halo3_wait(0)
-            weights_wait(2)
-
         @pl.when(half == 1)
         def _():
             for t in range(4):
                 start_all(load4(t))
 
-        stage_r2(0, 2 * half, 2, 0, 8)
 
     loop(2, per_image)
+    halo3_wait(0)
+    weights_wait(2)
+    stage_r2(0, 0, 4, 0, 8)
     halo4_start(0)
     halo3_wait(1)
     stage_r2(1, 0, 4, 4, 4)
@@ -461,6 +464,13 @@
     for t in (3, 4):
         start_all(load5(t))
 
+    def center_r3(t):
+        wait_all(load5(t))
+        lhs = y3v[:, 1:5].reshape(PART, TOP)
+        acc[t] = jnp.dot(lhs, wbuf[pl.ds(base5(t) + 4, 4)].reshape(TOP, WIDE), preferred_element_type=F32)
+
+    loop(3, center_r3)
+
     def finish(step):
         for i in range(2):
             @pl.when(jnp.logical_not(is_local(step, i)))
@@ -485,7 +495,10 @@
     loop(total // 3, halo_wait)
 
     def stage_r3(t):
-        wait_all(load5(t))
+        @pl.when(t >= 3)
+        def _():
+            wait_all(load5(t))
+
         ahead = t + 4
 
         @pl.when(jnp.logical_and(t >= 1, ahead < total))
@@ -494,9 +507,21 @@
 
         j = lax.rem(t, 3)
         n = t // 3
-        lhs = jnp.concatenate([y3v[:, dy : dy + 4].reshape(PART, TOP) for dy in range(3)], axis=1)
-        rhs = wbuf[pl.ds(base5(t), 12)].reshape(6144, WIDE)
-        acc[j] = jnp.dot(lhs, rhs, preferred_element_type=F32)
+
+        def rows_of(dy):
+            return y3v[:, dy : dy + 4].reshape(PART, TOP)
+
+        @pl.when(t < 3)
+        def _():
+            lhs = jnp.concatenate([rows_of(0), rows_of(2)], axis=1)
+            rhs = jnp.concatenate([wbuf[pl.ds(base5(t) + 8 * k, 4)].reshape(TOP, WIDE) for k in range(2)], axis=0)
+            acc[j] += jnp.dot(lhs, rhs, preferred_element_type=F32)
+
+        @pl.when(t >= 3)
+        def _():
+            lhs = jnp.concatenate([rows_of(dy) for dy in range(3)], axis=1)
+            rhs = wbuf[pl.ds(base5(t), 12)].reshape(6144, WIDE)
+            acc[j] = jnp.dot(lhs, rhs, preferred_element_type=F32)
 
         @pl.when(j == 2)
         def _():
@@ -569,7 +594,7 @@
     return pl.pallas_call(
         kernel,
         out_shape=jax.ShapeDtypeStruct((4, 2, 2, 16, TOP), BF16),
-        in_specs=[ANY_SPEC, VM_SPEC, VM_SPEC] + [ANY_SPEC] * 5 + [VM_SPEC] * 5,
+        in_specs=[ANY_SPEC, ANY_SPEC, VM_SPEC] + [ANY_SPEC] * 5 + [VM_SPEC] * 5,
         out_specs=ANY_SPEC,
         scratch_shapes=[
             VM((2, 2, 8, LANE, PART), BF16),
@@ -588,12 +613,12 @@
             VM((2, 6, 32, TOP), BF16),
             VM((3, PART, WIDE), F32),
         ]
-        + [SEM((n,)) for n in (2, 8, 8, 2, 2, 16, 16, 2, 5)]
+        + [SEM((n,)) for n in (2, 8, 8, 2, 2, 16, 16, 2, 6)]
         + [SEM((4,))] * 13
         + [SEM(n) for n in ((4, 3), (5, 3), (4, 8), (4, 8))],
         compiler_params=PARAMS,
         name="encoder",
-    )(images, w0.reshape(3, 768, WIDE), flat[0], w1.reshape(9, WIDE, WIDE), w2.reshape(9, WIDE, MID), w3.reshape(18, WIDE, MID), w4.reshape(3, 3, 2, WIDE, TOP), w5.reshape(3, 3, 4, WIDE, TOP), *flat[1:])
+    )(images, w0.reshape(9, PART, WIDE), flat[0], w1.reshape(9, WIDE, WIDE), w2.reshape(9, WIDE, MID), w3.reshape(18, WIDE, MID), w4.reshape(3, 3, 2, WIDE, TOP), w5.reshape(3, 3, 4, WIDE, TOP), *flat[1:])
 
 
 def solution(mesh):

time: 176 us -> 172 us (0.977)
  Pallas kernels: 171 us -> 169 us
    pallas_call x1, Pallas kernels: 171 us -> 169 us  [encoder(): pl.pallas_call(kernel, out_shape=jax.ShapeDtypeStruct((4, 2, 2, 16, TOP),...]
where the time goes in v3:
time: 172 us; the launch traced here: 171 us
  Pallas kernels  169 us (98%)
  local copies, waits for them, and re-layouts  2.3 us (1%)
    pallas_call x1, Pallas kernels, encoder(): pl.pallas_call(kernel, out_shape=jax.ShapeDtypeStruct((4, 2, 2, 16, TOP),...  169 us

profile of v3, /device:TPU:1, one launch (start us, length us, event | category | flops | bytes accessed | tf_op | source)
XLA Modules:
  0.0 170.9 jit_solution(655472493228870094)
XLA Ops:
  0.0 168.6 %encoder.1 = bf16[4,2,2,16,2048]{4,3,2,1,0:T(8,128)(2,1)} custom-call(bf16[16,8,128,256]{3,2,1,0:T(8,128)(2,1)} %refs_0_.1, bf16[9,256,512]{2,1,0:T(8,128)(2,1)} %bitcast.20, f32[1,512]{1,0:T(1,128)} %bitcast.25, bf16[9,512,512]{2,1,0:T(8,128)(2,1)} %bitcast.18, bf16[9,512,1024]{2,1,0:T(8,128)(2,1)} %bitcast.17, bf16[18,512,1024]{2,1,0:T(8,128)(2,1)} %bitcast.16, ...), custom_call_target="tpu_custom_call" | custom-call | tf_op jit(solution)/shard_map/encoder/pallas_call | solution.py:594
  168.6 2.3 %copy.16 = bf16[16,1,16,2048]{3,2,1,0:T(8,128)(2,1)} copy(bf16[16,1,16,2048]{3,2,1,0:T(8,128)(2,1)} %bitcast.19) | data formatting | bytes 2097152
